TPU v7x, 128 devices: a whole 4x4x4 slice. The times are simulated.
128 devices in a mesh: rows: 16 (over x, z), cols: 8 (over y, core).
Axes of the slice: x: 4, y: 4, z: 4, core: 2. Of those that a mesh axis runs over, the one named last changes fastest.
Arguments:
- margins: bfloat16 [16384, 2048], P(('rows', 'cols')), may hold values from -512 to 512
- subset_masks: bfloat16 [16384, 8192], P('rows'), may hold values from 0 to 1
- ridge_param: float32 [], replicated, may hold values from 2048 to 8192
Outputs:
- weights: float32 [8192, 2048], P('rows', 'cols')
- residual_norm: float32 [2048], P('cols')
All inputs are finite; a program needn't handle non-finite values.
Results may differ from a plain program's by a relative error of at most 0.0021.
Values may be sent and summed in bfloat16 or wider, within the bound.
A program may use at most 128 MiB of HBM per device.

v0:
```python
import jax
import jax.numpy as jnp
from jax import lax
from jax.sharding import PartitionSpec as P

ITERS = 2


def copy_for_each(array, axis):
    copies = jnp.broadcast_to(array, (lax.axis_size(axis), *array.shape))
    return lax.all_to_all(copies, axis, split_axis=0, concat_axis=0, tiled=True)


def over_copies(array, axis):
    everything = copy_for_each(array, axis)
    return jnp.sum(everything, axis=0)


def split_up(array, dim, size):
    dims = array.shape
    pieces = array.reshape(*dims[:dim], size, dims[dim] // size, *dims[dim + 1 :])
    return jnp.moveaxis(pieces, dim, 0)


def sent_and_summed(array, axis, dim):
    size = lax.axis_size(axis)
    pieces = lax.all_to_all(split_up(array, dim, size), axis, 0, 0, tiled=True)
    return jnp.sum(pieces.astype(jnp.float32), axis=0)


def per_device(margins, subset_masks, ridge_param):
    design = subset_masks * 2 - 1
    regrouped = lax.all_to_all(margins, "cols", split_axis=1, concat_axis=0, tiled=True)

    def design_times(operand):
        return lax.dot_general(
            design, operand, (((0,), (0,)), ((), ())), preferred_element_type=jnp.float32
        )

    target = lax.psum_scatter(design_times(regrouped), "rows", scatter_dimension=0, tiled=True)
    first_norms = lax.psum(jnp.sum(target * target, axis=0), "rows")
    weights = jnp.zeros_like(target)
    residual = target
    direction = target
    norm_now = first_norms
    for iteration in range(ITERS):
        dir_low = direction.astype(jnp.bfloat16)
        fitted = jnp.dot(
            design,
            lax.all_gather(dir_low, "rows", axis=0, tiled=True),
            preferred_element_type=jnp.float32,
        )
        fitted_low = fitted.astype(jnp.bfloat16)
        partial_sum = jnp.sum(fitted * fitted_low.astype(jnp.float32), axis=0)
        partial_sum = partial_sum + ridge_param * jnp.sum(
            dir_low.astype(jnp.float32) * direction, axis=0
        )
        curvature = over_copies(partial_sum, "rows")
        image = (
            sent_and_summed(design_times(fitted_low).astype(jnp.bfloat16), "rows", 0)
            + ridge_param * direction
        )
        alpha = norm_now / curvature
        weights = weights + alpha * direction
        residual = residual - alpha * image
        norm_next = over_copies(jnp.sum(residual * residual, axis=0), "rows")
        if iteration + 1 < ITERS:
            direction = residual + norm_next / norm_now * direction
        norm_now = norm_next
    return (weights, jnp.sqrt(norm_now / first_norms))


def solution(mesh):
    in_specs = (P(("rows", "cols"), None), P("rows", None), P())
    out_specs = (P("rows", "cols"), P("cols"))
    return jax.shard_map(
        per_device, mesh=mesh, in_specs=in_specs, out_specs=out_specs, check_vma=False
    )
```

profile of v0, /device:TPU:0, one launch (start us, length us, event | category | flops | bytes accessed | tf_op | source)
XLA Modules:
  0.0 482.3 jit_solution(14549520396129488273)
XLA Ops:
  7.2 0.0 reduce-scatter.2.cloned.1.call-start
  7.2 1.3 copy.9
  8.5 14.7 %all_to_all.53 = bf16[128,8,256]{0,2,1:T(8,128)(2,1)S(1)} all-to-all(bf16[128,8,256]{0,2,1:T(8,128)(2,1)S(1)} %bitcast.13), channel_id=1, replica_groups=mesh['rows'=16,'cols'=8] {'cols'}, dimensions={1} | all-to-all | bytes 1048576 | tf_op jit(solution)/shard_map/all_to_all | solution.py:33
  23.3 0.2 copy.10
  23.5 14.1 %fusion.2 = f32[8192,256]{1,0:T(8,128)} fusion(bf16[1024,256]{1,0:T(8,128)(2,1)S(1)} %bitcast.14, bf16[1024,8192]{1,0:T(8,128)(2,1)} %param.4), kind=kOutput, calls=%fused_computation.9 | convolution fusion | flops 4311744512 | bytes 25690112 | tf_op jit(solution)/shard_map/dot_general | solution.py:36
  37.6 0.0 reduce-scatter.2.cloned.1.call-update
  37.6 0.0 all-gather.3.cloned.1.call-start
  37.7 86.4 %reduce-scatter.2.cloned.1.call-done = f32[512,256]{1,0:T(8,128)} async-done(((f32[8192,256]{1,0:T(8,128)}), f32[512,256]{1,0:T(8,128)}) %reduce-scatter.2.cloned.1.call-update) | async-done | bytes 524304 | tf_op jit(solution)/shard_map/reduce_scatter | solution.py:40
  124.1 2.0 multiply_reduce_fusion.5
  126.0 0.0 all-gather.3.cloned.1.call-update
  126.7 50.9 %all-gather.3.cloned.1.call-done = bf16[8192,256]{1,0:T(8,128)(2,1)} async-done(((bf16[512,256]{1,0:T(8,128)(2,1)}), bf16[8192,256]{1,0:T(8,128)(2,1)}) %all-gather.3.cloned.1.call-update) | async-done | bytes 4194320 | tf_op jit(solution)/shard_map/all_gather | solution.py:50
  177.6 11.5 %multiply_reduce_fusion.1 = (f32[256]{0:T(256)S(1)}, bf16[1024,256]{1,0:T(8,128)(2,1)S(1)}) fusion(bf16[8192,256]{1,0:T(8,128)(2,1)} %all-gather.3.cloned.1.call-done, bf16[1024,8192]{1,0:T(8,128)(2,1)} %param.4), kind=kOutput, calls=%fused_computation.6 | convolution fusion | flops 4313055232 | bytes 21496832 | tf_op jit(solution)/shard_map/dot_general | solution.py:48
  189.1 0.6 broadcast_in_dim.8
  189.7 5.3 %all-to-all-start.1 = ((f32[16,1,256]{2,1,0:T(1,128)}), f32[16,1,256]{2,1,0:T(1,128)S(1)}, u32[]{:S(2)}, u32[]{:S(2)}) async-start(f32[16,1,256]{2,1,0:T(1,128)} %broadcast_in_dim.8), calls=%async_computation.2 | async-start | bytes 32768 | tf_op jit(solution)/shard_map/all_to_all | solution.py:11
  195.0 0.0 copy-start
  195.0 12.9 %convolution_convert_fusion.1 = bf16[8192,256]{1,0:T(8,128)(2,1)} fusion(bf16[1024,8192]{1,0:T(8,128)(2,1)} %param.4, bf16[1024,256]{1,0:T(8,128)(2,1)S(1)} %get-tuple-element.10), kind=kOutput, calls=%fused_computation.2 | convolution fusion | flops 4313841664 | bytes 21495808 | tf_op jit(solution)/shard_map/dot_general | solution.py:36
  207.8 0.0 all-to-all-done.1
  207.8 7.3 %all-to-all-start.2 = ((bf16[16,512,256]{2,1,0:T(8,128)(2,1)}), bf16[16,512,256]{2,1,0:T(8,128)(2,1)}, u32[]{:S(2)}, u32[]{:S(2)}) async-start(bf16[16,512,256]{2,1,0:T(8,128)(2,1)} %bitcast.10), calls=%async_computation.3 | async-start | bytes 8388608 | tf_op jit(solution)/shard_map/all_to_all | solution.py:27
  215.1 0.0 all-gather.5.cloned.1.call-start
  215.2 83.0 %psum.7 = f32[256]{0:T(256)S(1)} all-reduce(f32[256]{0:T(256)S(1)} %get-tuple-element.3), channel_id=1, replica_groups=mesh['rows'=16,'cols'=8] {'rows'}, use_global_device_ids=true, to_apply=%region_2.0 | all-reduce | flops 256 | bytes 2048 | tf_op jit(solution)/shard_map/psum | solution.py:41
  298.2 0.0 all-to-all-done.2
  298.2 2.8 convert_reduce_fusion.1
  301.1 0.0 copy-done
  301.1 0.2 multiply_reduce_fusion.4
  301.2 11.8 %all_to_all.54 = f32[16,1,256]{2,1,0:T(1,128)S(1)} all-to-all(f32[16,1,256]{2,1,0:T(1,128)S(1)} %broadcast_in_dim.18), channel_id=1, replica_groups=mesh['rows'=16,'cols'=8] {'rows'}, dimensions={0} | all-to-all | bytes 32768 | tf_op jit(solution)/shard_map/all_to_all | solution.py:11
  313.0 0.9 multiply_reduce_fusion.3
  313.9 0.0 all-gather.5.cloned.1.call-update
  313.9 49.2 %all-gather.5.cloned.1.call-done = bf16[8192,256]{1,0:T(8,128)(2,1)} async-done(((bf16[512,256]{1,0:T(8,128)(2,1)}), bf16[8192,256]{1,0:T(8,128)(2,1)}) %all-gather.5.cloned.1.call-update) | async-done | bytes 4194320 | tf_op jit(solution)/shard_map/all_gather | solution.py:50
  363.2 11.5 %multiply_reduce_fusion = (f32[256]{0:T(256)S(1)}, bf16[1024,256]{1,0:T(8,128)(2,1)S(1)}) fusion(bf16[8192,256]{1,0:T(8,128)(2,1)} %all-gather.5.cloned.1.call-done, bf16[1024,8192]{1,0:T(8,128)(2,1)} %param.4), kind=kOutput, calls=%fused_computation.5 | convolution fusion | flops 4313055232 | bytes 21496832 | tf_op jit(solution)/shard_map/dot_general | solution.py:48
  374.7 0.6 broadcast_in_dim.19
  375.3 5.3 %all-to-all-start.4 = ((f32[16,1,256]{2,1,0:T(1,128)}), f32[16,1,256]{2,1,0:T(1,128)S(1)}, u32[]{:S(2)}, u32[]{:S(2)}) async-start(f32[16,1,256]{2,1,0:T(1,128)} %broadcast_in_dim.19), calls=%async_computation.5 | async-start | bytes 32768 | tf_op jit(solution)/shard_map/all_to_all | solution.py:11
  380.6 12.8 %convolution_convert_fusion = bf16[8192,256]{1,0:T(8,128)(2,1)} fusion(bf16[1024,8192]{1,0:T(8,128)(2,1)} %param.4, bf16[1024,256]{1,0:T(8,128)(2,1)S(1)} %get-tuple-element.12), kind=kOutput, calls=%fused_computation.1 | convolution fusion | flops 4313841664 | bytes 21495808 | tf_op jit(solution)/shard_map/dot_general | solution.py:36
  393.4 0.0 all-to-all-done.4
  393.4 7.3 %all-to-all-start.5 = ((bf16[16,512,256]{2,1,0:T(8,128)(2,1)}), bf16[16,512,256]{2,1,0:T(8,128)(2,1)}, u32[]{:S(2)}, u32[]{:S(2)}) async-start(bf16[16,512,256]{2,1,0:T(8,128)(2,1)} %bitcast.11), calls=%async_computation.6 | async-start | bytes 8388608 | tf_op jit(solution)/shard_map/all_to_all | solution.py:27
  400.7 54.3 %all-to-all-done.5 = bf16[16,512,256]{2,1,0:T(8,128)(2,1)} async-done(((bf16[16,512,256]{2,1,0:T(8,128)(2,1)}), bf16[16,512,256]{2,1,0:T(8,128)(2,1)}, u32[]{:S(2)}, u32[]{:S(2)}) %all-to-all-start.5) | async-done | bytes 4194336 | tf_op jit(solution)/shard_map/all_to_all | solution.py:27
  455.0 2.8 convert_reduce_fusion
  457.8 1.1 multiply_reduce_fusion.2
  458.9 16.2 %all_to_all.55 = f32[16,1,256]{2,1,0:T(1,128)S(1)} all-to-all(f32[16,1,256]{2,1,0:T(1,128)S(1)} %broadcast_in_dim.20), channel_id=1, replica_groups=mesh['rows'=16,'cols'=8] {'rows'}, dimensions={0} | all-to-all | bytes 32768 | tf_op jit(solution)/shard_map/all_to_all | solution.py:11
  475.2 0.6 divide_sqrt_fusion
  (11 shorter events, 0.2 us)
Async XLA Ops:
  7.2 116.9 %reduce-scatter.2.cloned.1.call-start = ((), (), s32[]{:S(2)}) async-start(), calls=%async_computation.8 | async-start | bytes 8912896 | tf_op jit(solution)/shard_map/reduce_scatter | solution.py:40
  37.6 140.0 %all-gather.3.cloned.1.call-start = ((), (), s32[]{:S(2)}) async-start(), calls=%async_computation.9 | async-start | bytes 4456448 | tf_op jit(solution)/shard_map/all_gather | solution.py:50
  189.7 18.1 %all-to-all-start.1 = ((f32[16,1,256]{2,1,0:T(1,128)}), f32[16,1,256]{2,1,0:T(1,128)S(1)}, u32[]{:S(2)}, u32[]{:S(2)}) async-start(f32[16,1,256]{2,1,0:T(1,128)} %broadcast_in_dim.8), calls=%async_computation.2 | async-start | bytes 32768 | tf_op jit(solution)/shard_map/all_to_all | solution.py:11
  195.0 106.1 %copy-start = (f32[512,256]{1,0:T(8,128)S(1)}, f32[512,256]{1,0:T(8,128)}, u32[]{:S(2)}) copy-start(f32[512,256]{1,0:T(8,128)} %reduce-scatter.2.cloned.1.call-done) | copy-start | bytes 1572868
  207.8 90.4 %all-to-all-start.2 = ((bf16[16,512,256]{2,1,0:T(8,128)(2,1)}), bf16[16,512,256]{2,1,0:T(8,128)(2,1)}, u32[]{:S(2)}, u32[]{:S(2)}) async-start(bf16[16,512,256]{2,1,0:T(8,128)(2,1)} %bitcast.10), calls=%async_computation.3 | async-start | bytes 8388608 | tf_op jit(solution)/shard_map/all_to_all | solution.py:27
  215.1 148.1 %all-gather.5.cloned.1.call-start = ((), (), s32[]{:S(2)}) async-start(), calls=%async_computation.10 | async-start | bytes 4456448 | tf_op jit(solution)/shard_map/all_gather | solution.py:50
  375.3 18.1 %all-to-all-start.4 = ((f32[16,1,256]{2,1,0:T(1,128)}), f32[16,1,256]{2,1,0:T(1,128)S(1)}, u32[]{:S(2)}, u32[]{:S(2)}) async-start(f32[16,1,256]{2,1,0:T(1,128)} %broadcast_in_dim.19), calls=%async_computation.5 | async-start | bytes 32768 | tf_op jit(solution)/shard_map/all_to_all | solution.py:11
  393.4 61.6 %all-to-all-start.5 = ((bf16[16,512,256]{2,1,0:T(8,128)(2,1)}), bf16[16,512,256]{2,1,0:T(8,128)(2,1)}, u32[]{:S(2)}, u32[]{:S(2)}) async-start(bf16[16,512,256]{2,1,0:T(8,128)(2,1)} %bitcast.11), calls=%async_computation.6 | async-start | bytes 8388608 | tf_op jit(solution)/shard_map/all_to_all | solution.py:27
Sparse Core Ops, SparseCore 0:
  37.7 86.2 reduce-scatter.1
  126.8 50.7 all-gather.2
  314.1 49.0 all-gather.4
where the time goes:
time: 483 us; the launch traced here: 482 us
  waiting for transfers between devices  241 us (50%)
  blocking collectives  126 us (26%)
  matrix products  62.7 us (13%)
  starting transfers between devices  25.2 us (5%)
  between operations  14.5 us (3%)
  other arithmetic  10.5 us (2%)
    all_gather x2, waiting for transfers between devices, per_device(): lax.all_gather(dir_low, 'rows', axis=0, tiled=True)  100 us
    reduce_scatter x1, waiting for transfers between devices, per_device(): lax.psum_scatter(design_times(regrouped), 'rows', scatter_dimension=0, ti...  86.4 us
    psum x1, blocking collectives, per_device(): first_norms = lax.psum(jnp.sum(target * target, axis=0), 'rows')  83 us
    all_to_all x2, waiting for transfers between devices, sent_and_summed(): pieces = lax.all_to_all(split_up(array, dim, size), axis, 0, 0, tiled=True)  54.3 us
    dot_general x3, matrix products, design_times(): lax.dot_general(design, operand, (((0,), (0,)), ((), ())), preferred_elem...  39.8 us
    all_to_all x2, blocking collectives, copy_for_each(): return lax.all_to_all(copies, axis, split_axis=0, concat_axis=0, tiled=True)  28 us
    dot_general x2, matrix products, per_device(): jnp.dot(design, lax.all_gather(dir_low, 'rows', axis=0, tiled=True), pref...  22.9 us
    all_to_all x1, blocking collectives, per_device(): lax.all_to_all(margins, 'cols', split_axis=1, concat_axis=0, tiled=True)  14.7 us
  transfers between devices with their start and end apart: 7, of which 4 were waited for; matrix products, arithmetic and copies ran while one was open for 5% of the time, Pallas kernels for 0%

commit v1 on v0

v1 whole, which is shorter than its diff:
```python
import functools

import jax
import jax.numpy as jnp
from jax import lax
from jax.experimental import pallas as pl
from jax.experimental.pallas import tpu as pltpu
from jax.sharding import PartitionSpec as P

MESH = pl.DeviceIdType.MESH
BF16 = jnp.bfloat16
F32 = jnp.float32
SIDE = 4
LOADS = 8

FIRST_SLOT = ({2: 4, 0: 5, 1: 2, 3: 3}, {2: 2, 0: 3, 1: 4, 3: 5})
GATHER_ORDER = ((0, 1, 3, 2), (0, 3, 1, 2))
GATHER_PASS = ((0, 3), (1, 2))


def fit(
    cols_size, ridge_ref, margins_ref, mask_ref, w_ref, rn_ref,
    design, regrouped, dir_all, image_all, fit_one, fit_two, fit_low, own, target, image,
    wide_s1, wide_r1, wide_s2, wide_r2, low_s1, low_r1, low_s2, low_r2, ex_s, ex_r,
    load_sem, m_send, m_recv, s1_send, s1_recv, s2_send, s2_recv,
    a1_send, a1_recv, a2_send, a2_recv, ex_send, ex_recv,
):
    row = lax.axis_index("rows")
    col = lax.axis_index("cols")
    x, z = lax.div(row, SIDE), lax.rem(row, SIDE)
    depth, examples = design.shape
    block = examples // (SIDE * SIDE)
    half = block // 2
    quarter = half // 2
    evals = target.shape[1]
    per = depth // cols_size
    ridge = ridge_ref[0, 0]

    def row_of(h, u1, u2):
        return lax.rem(u1 + 8, SIDE) * (4 - 3 * h) + lax.rem(u2 + 8, SIDE) * (1 + 3 * h)

    def c1(h):
        return x * (1 - h) + z * h

    def c2(h):
        return z * (1 - h) + x * h

    def first(h, u1, u2):
        return pl.multiple_of(row_of(h, u1, u2) * block + h * half, half)

    def load(i):
        rows = pl.ds(i * (depth // LOADS), depth // LOADS)
        return pltpu.make_async_copy(mask_ref.at[rows], design.at[rows], load_sem.at[i])

    def line(i):
        return lax.rem(x + i, SIDE) * SIDE + z, x * SIDE + lax.rem(z + i, SIDE)

    for i in range(LOADS):
        load(i).start()

    barrier = pltpu.get_barrier_semaphore()
    for i in range(1, SIDE):
        for peer in line(i):
            pl.semaphore_signal(barrier, inc=1, device_id={"rows": peer}, device_id_type=MESH)
    for i in range(1, cols_size):
        peer = lax.rem(col + i, cols_size)
        pl.semaphore_signal(barrier, inc=1, device_id={"cols": peer}, device_id_type=MESH)
    pl.semaphore_wait(barrier, 2 * (SIDE - 1) + cols_size - 1)

    def hand_over(i):
        peer = lax.rem(col + i, cols_size)
        return pltpu.make_async_remote_copy(
            margins_ref.at[:, pl.ds(pl.multiple_of(peer * evals, evals), evals)],
            regrouped.at[pl.ds(pl.multiple_of(col * per, per), per)],
            m_send.at[i - 1],
            m_recv.at[i - 1],
            device_id={"cols": peer},
            device_id_type=MESH,
        )

    for i in range(1, cols_size):
        hand_over(i).start()
    regrouped[pl.ds(pl.multiple_of(col * per, per), per)] = margins_ref[
        :, pl.ds(pl.multiple_of(col * evals, evals), evals)
    ]

    step = min(16, depth // LOADS)
    for i in range(LOADS):
        load(i).wait()

        @pl.loop(0, depth // LOADS // step)
        def _(j):
            rows = pl.ds(pl.multiple_of(i * (depth // LOADS) + j * step, step), step)
            design[rows] = design[rows] * 2 - 1

    for i in range(1, cols_size):
        hand_over(i).wait()

    def partial(operand, h, u1, u2):
        return lax.dot_general(
            design[:, pl.ds(first(h, u1, u2), half)],
            operand[...],
            (((0,), (0,)), ((), ())),
            preferred_element_type=F32,
        )

    def reduce_scatter(operand, s1, r1, s2, r2, after_far, after_own, done):
        kind = s1.dtype

        def send1(h, d, slot):
            return pltpu.make_async_remote_copy(
                s1.at[h, d, slot],
                r1.at[h, d, slot],
                s1_send.at[h, d, slot],
                s1_recv.at[h, d, slot],
                device_id={"rows": row_of(h, c1(h) + 1 - 2 * d, c2(h))},
                device_id_type=MESH,
            )

        def send2(h, d, slot):
            return pltpu.make_async_remote_copy(
                s2.at[h, d, slot],
                r2.at[h, d, slot],
                s2_send.at[h, d, slot],
                s2_recv.at[h, d, slot],
                device_id={"rows": row_of(h, c1(h), c2(h) + 1 - 2 * d)},
                device_id_type=MESH,
            )

        def parts(i):
            return lax.rem(i, 2), lax.rem(lax.div(i, 2), 2), lax.div(i, 4)

        @pl.loop(0, 8)
        def _(i):
            h, d, s = parts(i)
            k = (2 - d) * (1 - s) + 3 * d * s
            s1[h, d, s] = partial(operand, h, c1(h) + 2, c2(h) + k).astype(kind)
            send1(h, d, s).start()

        @pl.loop(0, 8)
        def _(i):
            h, d, s = parts(i)
            k = (1 + d) * (1 - s) + 3 * (1 - d) * s
            s1[h, d, 2 + s] = partial(operand, h, c1(h) + 1 - 2 * d, c2(h) + k).astype(kind)
            send1(h, d, 2 + s).start()

        after_far()

        @pl.loop(0, 8)
        def _(i):
            h, d, s = parts(i)
            k = (2 - d) * (1 - s) + 3 * d * s
            here = partial(operand, h, c1(h) + 1 - 2 * d, c2(h) + k)
            send1(h, d, s).wait_recv()
            s1[h, d, 4 + s] = (here + r1[h, d, s].astype(F32)).astype(kind)
            send1(h, d, 4 + s).start()

        @pl.loop(0, 8)
        def _(i):
            h, k = lax.rem(i, 2), lax.div(i, 2)
            own[h, k] = partial(operand, h, c1(h), c2(h) + k)

        after_own()

        def collect(h, k):
            for d in (0, 1):
                send1(h, d, FIRST_SLOT[d][k]).wait_recv()
            own[h, k] = (
                own[h, k]
                + r1[h, 0, FIRST_SLOT[0][k]].astype(F32)
                + r1[h, 1, FIRST_SLOT[1][k]].astype(F32)
            )

        def part(h, k, j):
            return own[h, k, pl.ds(j * quarter, quarter)]

        for h in (0, 1):
            collect(h, 2)
            for d in (0, 1):
                s2[h, d, 0] = part(h, 2, d).astype(kind)
                send2(h, d, 0).start()
        for d, k in ((0, 1), (1, 3)):
            for h in (0, 1):
                collect(h, k)
                s2[h, d, 1] = part(h, k, 1 - d).astype(kind)
                send2(h, d, 1).start()
        for h in (0, 1):
            for d, k in ((0, 1), (1, 3)):
                send2(h, d, 0).wait_recv()
                s2[h, d, 2] = (part(h, k, d) + r2[h, d, 0].astype(F32)).astype(kind)
                send2(h, d, 2).start()
        for h in (0, 1):
            collect(h, 0)
        for h in (0, 1):
            sums = []
            for j in (0, 1):
                send2(h, j, 2).wait_recv()
                send2(h, 1 - j, 1).wait_recv()
                sums.append(
                    part(h, 0, j) + r2[h, j, 2].astype(F32) + r2[h, 1 - j, 1].astype(F32)
                )
            done(h, sums)

        def drain():
            @pl.loop(0, 24)
            def _(i):
                send1(lax.rem(i, 2), lax.rem(lax.div(i, 2), 2), lax.div(i, 4)).wait_send()

            @pl.loop(0, 12)
            def _(i):
                send2(lax.rem(i, 2), lax.rem(lax.div(i, 2), 2), lax.div(i, 4)).wait_send()

        return drain

    def gather_steps(everything):
        def copy(rows, sends, recvs, h, d, slot, peer):
            return pltpu.make_async_remote_copy(
                everything.at[rows],
                everything.at[rows],
                sends.at[h, d, slot],
                recvs.at[h, d, slot],
                device_id={"rows": peer},
                device_id_type=MESH,
            )

        def send1(h, d, slot):
            sign = 1 - 2 * d
            if slot == 0:
                rows = pl.ds(first(h, c1(h), c2(h)), half)
            else:
                start = first(h, c1(h), c2(h) - sign) + d * quarter
                rows = pl.ds(pl.multiple_of(start, quarter), quarter)
            return copy(rows, a1_send, a1_recv, h, d, slot, row_of(h, c1(h), c2(h) + sign))

        def send2(h, d, slot):
            sign = 1 - 2 * d
            if slot < 4:
                rows = pl.ds(first(h, c1(h), c2(h) + GATHER_ORDER[d][slot]), half)
            else:
                rows = pl.ds(first(h, c1(h) - sign, c2(h) + GATHER_PASS[d][slot - 4]), half)
            return copy(rows, a2_send, a2_recv, h, d, slot, row_of(h, c1(h) + sign, c2(h)))

        return send1, send2

    def gather_start(everything, h):
        send1, send2 = gather_steps(everything)
        for d in (0, 1):
            send1(h, d, 0).start()
        for d in (0, 1):
            send2(h, d, 0).start()

    def gather_and_multiply(everything, result, meanwhile):
        send1, send2 = gather_steps(everything)
        tile = min(256, depth)

        def multiply(places, fresh=False):
            starts = [first(h, c1(h) + u1, c2(h) + u2) for h in (0, 1) for u1, u2 in places]

            @pl.loop(0, depth // tile)
            def _(i):
                rows = pl.ds(pl.multiple_of(i * tile, tile), tile)
                total = None
                for start in starts:
                    term = jnp.dot(
                        design[rows, pl.ds(start, half)],
                        everything[pl.ds(start, half)],
                        preferred_element_type=F32,
                    )
                    total = term if total is None else total + term
                result[rows] = total if fresh else result[rows] + total

        multiply([(0, 0)], fresh=True)
        for h in (0, 1):
            for d in (0, 1):
                send1(h, d, 0).wait_recv()
                send1(h, d, 1).start()
        for h in (0, 1):
            for slot in (1, 2):
                for d in (0, 1):
                    send2(h, d, slot).start()
        meanwhile[0]()
        multiply([(0, 1), (0, 3)])
        for h in (0, 1):
            for d in (0, 1):
                send1(h, d, 1).wait_recv()
            for d in (0, 1):
                send2(h, d, 3).start()
        multiply([(0, 2)])
        meanwhile[1]()
        for h in (0, 1):
            for d in (0, 1):
                send2(h, d, 0).wait_recv()
            send2(h, 0, 4).start()
        multiply([(-1, 0), (1, 0)])
        for h in (0, 1):
            for slot in (1, 2):
                for d in (0, 1):
                    send2(h, d, slot).wait_recv()
            send2(h, 0, 5).start()
            send2(h, 1, 4).start()
        multiply([(-1, 1), (1, 3)])
        multiply([(-1, 3), (1, 1)])
        for h in (0, 1):
            for d in (0, 1):
                send2(h, d, 3).wait_recv()
            send2(h, 1, 5).start()
        multiply([(-1, 2), (1, 2)])
        meanwhile[2]()
        for slot in (4, 5):
            for h in (0, 1):
                for d in (0, 1):
                    send2(h, d, slot).wait_recv()
            multiply([(2, GATHER_PASS[0][slot - 4]), (2, GATHER_PASS[1][slot - 4])])
        for h in (0, 1):
            for d in (0, 1):
                for slot in range(2):
                    send1(h, d, slot).wait_send()
                for slot in range(6):
                    send2(h, d, slot).wait_send()

    def exchange(e, stage, i):
        return pltpu.make_async_remote_copy(
            ex_s.at[e, stage],
            ex_r.at[e, stage, i - 1],
            ex_send.at[e, stage, i - 1],
            ex_recv.at[e, stage, i - 1],
            device_id={"rows": line(i)[stage]},
            device_id_type=MESH,
        )

    def exchange_start(e, stage):
        for i in range(1, SIDE):
            exchange(e, stage, i).start()

    def exchange_sum(e, stage):
        total = ex_s[e, stage]
        for i in range(1, SIDE):
            exchange(e, stage, i).wait()
            total = total + ex_r[e, stage, i - 1]
        return total

    def exchange_turn(e):
        ex_s[e, 1] = exchange_sum(e, 0)
        exchange_start(e, 1)

    def total(values):
        return jnp.sum(values, axis=0, keepdims=True)

    def low(values):
        return values.astype(BF16).astype(F32)

    def nothing():
        pass

    def keep(store, everything):
        def done(h, sums):
            for j in (0, 1):
                rows = pl.ds(h * half + j * quarter, quarter)
                store[rows] = sums[j]
                at = pl.multiple_of(row * block + h * half + j * quarter, quarter)
                everything[pl.ds(at, quarter)] = sums[j].astype(BF16)
            gather_start(everything, h)

        return done

    drain = reduce_scatter(
        regrouped, wide_s1, wide_r1, wide_s2, wide_r2, nothing, nothing, keep(target, dir_all)
    )
    gather_and_multiply(dir_all, fit_one, (nothing, drain, nothing))

    fit_low[...] = fit_one[...].astype(BF16)

    ex_s[0, 0] = jnp.zeros_like(ex_s[0, 0])
    ex_s[0, 0, pl.ds(0, 1)] = total(target[...] * target[...])
    ex_s[0, 0, pl.ds(1, 1)] = total(fit_one[...] * fit_low[...].astype(F32)) + ridge * total(
        low(target[...]) * target[...]
    )
    exchange_start(0, 0)

    drain = reduce_scatter(
        fit_low, low_s1, low_r1, low_s2, low_r2,
        functools.partial(exchange_turn, 0), nothing, keep(image, image_all),
    )
    sums = exchange_sum(0, 1)
    first_norms = sums[0:1]
    alpha_one = first_norms / sums[1:2]

    def residual_one():
        return target[...] - alpha_one * (image[...] + ridge * target[...])

    ex_s[1, 0] = jnp.zeros_like(ex_s[1, 0])
    ex_s[1, 0, pl.ds(0, 1)] = total(residual_one() * residual_one())
    exchange_start(1, 0)

    def middle():
        exchange_turn(1)
        drain()

    gather_and_multiply(image_all, fit_two, (nothing, middle, nothing))
    norm_one = exchange_sum(1, 1)[0:1]
    beta = norm_one / first_norms
    fit_two[...] = (1 + beta - alpha_one * ridge) * fit_one[...] - alpha_one * fit_two[...]
    fit_low[...] = fit_two[...].astype(BF16)

    ex_s[2, 0] = jnp.zeros_like(ex_s[2, 0])
    residual = residual_one()
    direction = residual + beta * target[...]
    w_ref[...] = alpha_one * target[...]
    image[...] = residual
    target[...] = direction
    ex_s[2, 0, pl.ds(0, 1)] = total(fit_two[...] * fit_low[...].astype(F32)) + ridge * total(
        low(target[...]) * target[...]
    )
    exchange_start(2, 0)

    def second_weights():
        alpha_two = norm_one / exchange_sum(2, 1)[0:1]
        ex_s[3, 1, pl.ds(0, 1)] = alpha_two
        w_ref[...] = w_ref[...] + alpha_two * target[...]

    def residual_two(h, sums):
        alpha_two = ex_s[3, 1, pl.ds(0, 1)]
        squares = None
        for j in (0, 1):
            rows = pl.ds(h * half + j * quarter, quarter)
            left = image[rows] - alpha_two * (sums[j] + ridge * target[rows])
            square = total(left * left)
            squares = square if squares is None else squares + square
        ex_s[3, 0, pl.ds(h, 1)] = squares

    ex_s[3, 0] = jnp.zeros_like(ex_s[3, 0])
    drain = reduce_scatter(
        fit_low, low_s1, low_r1, low_s2, low_r2,
        functools.partial(exchange_turn, 2), second_weights, residual_two,
    )
    exchange_start(3, 0)
    exchange_turn(3)
    drain()
    squares = exchange_sum(3, 1)
    rn_ref[...] = jnp.sqrt((squares[0:1] + squares[1:2]) / first_norms)


def per_device(cols_size, margins, subset_masks, ridge_param):
    depth, examples = subset_masks.shape
    evals = margins.shape[1] // cols_size
    block = examples // (SIDE * SIDE)
    half, quarter = block // 2, block // 4
    vmem = pl.BlockSpec(memory_space=pltpu.VMEM)
    first = (2, 2, 6, half, evals)
    second = (2, 2, 3, quarter, evals)
    weights, norms = pl.pallas_call(
        functools.partial(fit, cols_size),
        out_shape=(
            jax.ShapeDtypeStruct((block, evals), F32),
            jax.ShapeDtypeStruct((1, evals), F32),
        ),
        in_specs=[
            pl.BlockSpec(memory_space=pltpu.SMEM),
            vmem,
            pl.BlockSpec(memory_space=pl.ANY),
        ],
        out_specs=(vmem, vmem),
        scratch_shapes=[
            pltpu.VMEM((depth, examples), BF16),
            pltpu.VMEM((depth, evals), BF16),
            pltpu.VMEM((examples, evals), BF16),
            pltpu.VMEM((examples, evals), BF16),
            pltpu.VMEM((depth, evals), F32),
            pltpu.VMEM((depth, evals), F32),
            pltpu.VMEM((depth, evals), BF16),
            pltpu.VMEM((2, SIDE, half, evals), F32),
            pltpu.VMEM((block, evals), F32),
            pltpu.VMEM((block, evals), F32),
            pltpu.VMEM(first, F32),
            pltpu.VMEM(first, F32),
            pltpu.VMEM(second, F32),
            pltpu.VMEM(second, F32),
            pltpu.VMEM(first, BF16),
            pltpu.VMEM(first, BF16),
            pltpu.VMEM(second, BF16),
            pltpu.VMEM(second, BF16),
            pltpu.VMEM((4, 2, 8, evals), F32),
            pltpu.VMEM((4, 2, SIDE - 1, 8, evals), F32),
            pltpu.SemaphoreType.DMA((LOADS,)),
            pltpu.SemaphoreType.DMA((max(cols_size - 1, 1),)),
            pltpu.SemaphoreType.DMA((max(cols_size - 1, 1),)),
            pltpu.SemaphoreType.DMA((2, 2, 6)),
            pltpu.SemaphoreType.DMA((2, 2, 6)),
            pltpu.SemaphoreType.DMA((2, 2, 3)),
            pltpu.SemaphoreType.DMA((2, 2, 3)),
            pltpu.SemaphoreType.DMA((2, 2, 2)),
            pltpu.SemaphoreType.DMA((2, 2, 2)),
            pltpu.SemaphoreType.DMA((2, 2, 6)),
            pltpu.SemaphoreType.DMA((2, 2, 6)),
            pltpu.SemaphoreType.DMA((4, 2, SIDE - 1)),
            pltpu.SemaphoreType.DMA((4, 2, SIDE - 1)),
        ],
        compiler_params=pltpu.CompilerParams(
            collective_id=0, has_side_effects=True, vmem_limit_bytes=66_000_000
        ),
    )(ridge_param.reshape(1, 1), margins, subset_masks)
    return weights, norms.reshape(evals)


def solution(mesh):
    in_specs = (P(("rows", "cols"), None), P("rows", None), P())
    out_specs = (P("rows", "cols"), P("cols"))
    return jax.shard_map(
        functools.partial(per_device, mesh.shape["cols"]),
        mesh=mesh, in_specs=in_specs, out_specs=out_specs, check_vma=False,
    )
```

time: 483 us -> 179 us (0.37)
  waiting for transfers between devices: 241 us -> 0 us
  Pallas kernels: 0 us -> 174 us
  blocking collectives: 126 us -> 0 us
  matrix products: 62.7 us -> 0 us
  starting transfers between devices: 25.2 us -> 0 us
  between operations: 14.5 us -> 1.29 us
  other arithmetic: 10.5 us -> 0 us
    pallas_call x0 -> x1, Pallas kernels: none -> 174 us  [per_device(): pl.pallas_call(functools.partial(fit, cols_size), out_shape=(jax.ShapeDty...]
    all_gather x2 -> x0, waiting for transfers between devices: 100 us -> none  [per_device(): lax.all_gather(dir_low, 'rows', axis=0, tiled=True)]
    reduce_scatter x1 -> x0, waiting for transfers between devices: 86.4 us -> none  [per_device(): lax.psum_scatter(design_times(regrouped), 'rows', scatter_dimension=0, ti...]
    psum x1 -> x0, blocking collectives: 83 us -> none  [per_device(): first_norms = lax.psum(jnp.sum(target * target, axis=0), 'rows')]
    dot_general x5 -> x0, matrix products: 62.7 us -> none  [the longest x3 39.8 us: design_times(): lax.dot_general(design, operand, (((0,), (0,)), ((), ())), preferred_elem...]
    all_to_all x4 -> x0, waiting for transfers between devices: 54.3 us -> none  [the longest x2 54.3 us: sent_and_summed(): pieces = lax.all_to_all(split_up(array, dim, size), axis, 0, 0, tiled=True)]
    all_to_all x3 -> x0, blocking collectives: 42.7 us -> none  [the longest x2 28 us: copy_for_each(): return lax.all_to_all(copies, axis, split_axis=0, concat_axis=0, tiled=True)]
    all_to_all x4 -> x0, starting transfers between devices: 25 us -> none  [the longest x2 14.5 us: sent_and_summed(): pieces = lax.all_to_all(split_up(array, dim, size), axis, 0, 0, tiled=True)]
  transfers between devices with their start and end apart: 7 -> 0, of which waited for: 4 -> 0; matrix products, arithmetic and copies ran while one was open for 5% -> 0% of each run, Pallas kernels for 0% -> 0%
where the time goes in v1:
time: 179 us; the launch traced here: 178 us
  Pallas kernels  174 us (97%)
  local copies, waits for them, and re-layouts  3.07 us (2%)
    pallas_call x1, Pallas kernels, per_device(): pl.pallas_call(functools.partial(fit, cols_size), out_shape=(jax.ShapeDty...  174 us

profile of v1, /device:TPU:0, one launch (start us, length us, event | category | flops | bytes accessed | tf_op | source)
XLA Modules:
  0.0 178.3 jit_solution(15576698092390399201)
XLA Ops:
  1.3 173.9 %shard_map.50 = (f32[512,256]{1,0:T(8,128)}, f32[1,256]{1,0:T(1,128)}) custom-call(f32[1,1]{1,0:T(1,128)} %bitcast.2.ridge_ref, bf16[128,2048]{1,0:T(8,128)(2,1)} %margins_ref.1, bf16[1024,8192]{1,0:T(8,128)(2,1)} %mask_ref.1), custom_call_target="tpu_custom_call" | custom-call | tf_op jit(solution)/shard_map/pallas_call | solution.py:451
  175.2 1.9 %copy.8 = f32[512,256]{1,0:T(8,128)} copy(f32[512,256]{1,0:T(8,128)} %get-tuple-element.8) | data formatting | bytes 1048576
  177.1 1.2 copy.9

commit v2 on v1

--- a/solution.py
+++ b/solution.py
@@ -13,16 +13,17 @@
 SIDE = 4
 LOADS = 8
 
-FIRST_SLOT = ({2: 4, 0: 5, 1: 2, 3: 3}, {2: 2, 0: 3, 1: 4, 3: 5})
+FIRST_SLOT = ({2: 2, 1: 1, 3: 4, 0: 5}, {2: 0, 1: 3, 3: 4, 0: 5})
+SPAN = 2.0**15.75
 GATHER_ORDER = ((0, 1, 3, 2), (0, 3, 1, 2))
 GATHER_PASS = ((0, 3), (1, 2))
 
 
 def fit(
-    cols_size, ridge_ref, margins_ref, mask_ref, w_ref, rn_ref,
+    cols_size, ridge_ref, margins_hbm, mask_ref, w_ref, rn_ref,
     design, regrouped, dir_all, image_all, fit_one, fit_two, fit_low, own, target, image,
-    wide_s1, wide_r1, wide_s2, wide_r2, low_s1, low_r1, low_s2, low_r2, ex_s, ex_r,
-    load_sem, m_send, m_recv, s1_send, s1_recv, s2_send, s2_recv,
+    s1, r1, s2, r2, ex_s, ex_r, margins,
+    load_sem, margins_sem, m_send, m_recv, s1_send, s1_recv, s2_send, s2_recv,
     a1_send, a1_recv, a2_send, a2_recv, ex_send, ex_recv,
 ):
     row = lax.axis_index("rows")
@@ -55,6 +56,8 @@
     def line(i):
         return lax.rem(x + i, SIDE) * SIDE + z, x * SIDE + lax.rem(z + i, SIDE)
 
+    margins_load = pltpu.make_async_copy(margins_hbm, margins, margins_sem)
+    margins_load.start()
     for i in range(LOADS):
         load(i).start()
 
@@ -70,7 +73,7 @@
     def hand_over(i):
         peer = lax.rem(col + i, cols_size)
         return pltpu.make_async_remote_copy(
-            margins_ref.at[:, pl.ds(pl.multiple_of(peer * evals, evals), evals)],
+            margins.at[:, pl.ds(pl.multiple_of(peer * evals, evals), evals)],
             regrouped.at[pl.ds(pl.multiple_of(col * per, per), per)],
             m_send.at[i - 1],
             m_recv.at[i - 1],
@@ -78,9 +81,10 @@
             device_id_type=MESH,
         )
 
+    margins_load.wait()
     for i in range(1, cols_size):
         hand_over(i).start()
-    regrouped[pl.ds(pl.multiple_of(col * per, per), per)] = margins_ref[
+    regrouped[pl.ds(pl.multiple_of(col * per, per), per)] = margins[
         :, pl.ds(pl.multiple_of(col * evals, evals), evals)
     ]
 
@@ -104,9 +108,7 @@
             preferred_element_type=F32,
         )
 
-    def reduce_scatter(operand, s1, r1, s2, r2, after_far, after_own, done):
-        kind = s1.dtype
-
+    def reduce_scatter(operand, encode, decode, after_far, after_own, done):
         def send1(h, d, slot):
             return pltpu.make_async_remote_copy(
                 s1.at[h, d, slot],
@@ -130,46 +132,52 @@
         def parts(i):
             return lax.rem(i, 2), lax.rem(lax.div(i, 2), 2), lax.div(i, 4)
 
+        def send_block(h, d, slot, far, k, add, source):
+            target = c1(h) + 2 * far + (1 - far) * (1 - 2 * d)
+            here = partial(operand, h, target, c2(h) + k)
+
+            if add is None:
+                s1[h, d, slot] = encode(here, 1, h, d, 0)
+            else:
+
+                @pl.when(add == 1)
+                def _():
+                    send1(h, d, source).wait_recv()
+                    there = decode(r1[h, d, source], 1, h, d, 0)
+                    s1[h, d, slot] = encode(here + there, 1, h, d, 1)
+
+                @pl.when(add == 0)
+                def _():
+                    s1[h, d, slot] = encode(here, 1, h, d, 0)
+
+            send1(h, d, slot).start()
+
         @pl.loop(0, 8)
         def _(i):
             h, d, s = parts(i)
-            k = (2 - d) * (1 - s) + 3 * d * s
-            s1[h, d, s] = partial(operand, h, c1(h) + 2, c2(h) + k).astype(kind)
-            send1(h, d, s).start()
-
-        @pl.loop(0, 8)
-        def _(i):
-            h, d, s = parts(i)
-            k = (1 + d) * (1 - s) + 3 * (1 - d) * s
-            s1[h, d, 2 + s] = partial(operand, h, c1(h) + 1 - 2 * d, c2(h) + k).astype(kind)
-            send1(h, d, 2 + s).start()
-
-        after_far()
-
-        @pl.loop(0, 8)
-        def _(i):
-            h, d, s = parts(i)
-            k = (2 - d) * (1 - s) + 3 * d * s
-            here = partial(operand, h, c1(h) + 1 - 2 * d, c2(h) + k)
-            send1(h, d, s).wait_recv()
-            s1[h, d, 4 + s] = (here + r1[h, d, s].astype(F32)).astype(kind)
-            send1(h, d, 4 + s).start()
+            send_block(h, d, s, 1 - (s - d) * (s - d), 2 - s, None, None)
 
         @pl.loop(0, 8)
         def _(i):
             h, k = lax.rem(i, 2), lax.div(i, 2)
             own[h, k] = partial(operand, h, c1(h), c2(h) + k)
 
+        after_far()
+
+        @pl.loop(0, 8)
+        def _(i):
+            h, d, s = parts(i)
+            add = 1 - (s - d) * (s - d)
+            send_block(h, d, 2 + s, 1 - add, d + 2 * (1 - s), add, d)
+
         after_own()
 
         def collect(h, k):
             for d in (0, 1):
-                send1(h, d, FIRST_SLOT[d][k]).wait_recv()
-            own[h, k] = (
-                own[h, k]
-                + r1[h, 0, FIRST_SLOT[0][k]].astype(F32)
-                + r1[h, 1, FIRST_SLOT[1][k]].astype(F32)
-            )
+                slot = FIRST_SLOT[d][k]
+                summed = int((d, slot) in ((0, 2), (0, 5), (1, 3), (1, 4)))
+                send1(h, d, slot).wait_recv()
+                own[h, k] = own[h, k] + decode(r1[h, d, slot], 1, h, d, summed)
 
         def part(h, k, j):
             return own[h, k, pl.ds(j * quarter, quarter)]
@@ -177,17 +185,25 @@
         for h in (0, 1):
             collect(h, 2)
             for d in (0, 1):
-                s2[h, d, 0] = part(h, 2, d).astype(kind)
+                s2[h, d, 0] = encode(part(h, 2, d), 2, h, d, 0)
                 send2(h, d, 0).start()
+
+        @pl.loop(0, 8)
+        def _(i):
+            h, d, s = parts(i)
+            add = s + d - 2 * s * d
+            send_block(h, d, 4 + s, s * 0, 3 * (1 - s), add, 3 - d)
+
         for d, k in ((0, 1), (1, 3)):
             for h in (0, 1):
                 collect(h, k)
-                s2[h, d, 1] = part(h, k, 1 - d).astype(kind)
+                s2[h, d, 1] = encode(part(h, k, 1 - d), 2, h, d, 0)
                 send2(h, d, 1).start()
-        for h in (0, 1):
-            for d, k in ((0, 1), (1, 3)):
+        for d, k in ((0, 1), (1, 3)):
+            for h in (0, 1):
                 send2(h, d, 0).wait_recv()
-                s2[h, d, 2] = (part(h, k, d) + r2[h, d, 0].astype(F32)).astype(kind)
+                there = decode(r2[h, d, 0], 2, h, d, 0)
+                s2[h, d, 2] = encode(part(h, k, d) + there, 2, h, d, 1)
                 send2(h, d, 2).start()
         for h in (0, 1):
             collect(h, 0)
@@ -197,7 +213,9 @@
                 send2(h, j, 2).wait_recv()
                 send2(h, 1 - j, 1).wait_recv()
                 sums.append(
-                    part(h, 0, j) + r2[h, j, 2].astype(F32) + r2[h, 1 - j, 1].astype(F32)
+                    part(h, 0, j)
+                    + decode(r2[h, j, 2], 2, h, j, 1)
+                    + decode(r2[h, 1 - j, 1], 2, h, 1 - j, 0)
                 )
             done(h, sums)
 
@@ -251,7 +269,7 @@
 
     def gather_and_multiply(everything, result, meanwhile):
         send1, send2 = gather_steps(everything)
-        tile = min(256, depth)
+        tile = depth
 
         def multiply(places, fresh=False):
             starts = [first(h, c1(h) + u1, c2(h) + u2) for h in (0, 1) for u1, u2 in places]
@@ -324,7 +342,7 @@
             ex_r.at[e, stage, i - 1],
             ex_send.at[e, stage, i - 1],
             ex_recv.at[e, stage, i - 1],
-            device_id={"rows": line(i)[stage]},
+            device_id={"rows": line(i)[stage if e < 5 else 1 - stage]},
             device_id_type=MESH,
         )
 
@@ -363,8 +381,46 @@
 
         return done
 
+    bound = jnp.max(jnp.abs(regrouped[...].astype(F32)), axis=0, keepdims=True) * depth
+    for e in (4, 5):
+        ex_s[e, 0] = jnp.broadcast_to(jnp.maximum(bound, 1e-30), ex_s.shape[2:])
+        exchange_start(e, 0)
+
+    def bounds_turn():
+        for e in (4, 5):
+            exchange_turn(e)
+
+    def bounds_end():
+        for e in (4, 5):
+            for i in range(1, SIDE):
+                exchange(e, 1, i).wait()
+
+    def sender_bound(stage, h, d, summed, here):
+        e = 4 + h
+        if here:
+            limit = ex_s[e, stage - 1, pl.ds(0, 1)]
+            return limit + ex_r[e, stage - 1, 2 * d, pl.ds(0, 1)] if summed else limit
+        limit = ex_r[e, stage - 1, 2 * d, pl.ds(0, 1)]
+        return limit + ex_r[e, stage - 1, 1, pl.ds(0, 1)] if summed else limit
+
+    def power_code(values, stage, h, d, summed):
+        q = values * (SPAN / sender_bound(stage, h, d, summed, True))
+        q2 = q * q
+        return ((q * jnp.abs(q)) * q2 * (q2 * q2)).astype(BF16)
+
+    def power_decode(values, stage, h, d, summed):
+        y = values.astype(F32)
+        root = jnp.exp(jnp.log(jnp.maximum(jnp.abs(y), 2.0**-126)) * 0.125)
+        return jnp.where(y < 0, -root, root) * (sender_bound(stage, h, d, summed, False) / SPAN)
+
+    def plain_code(values, stage, h, d, summed):
+        return values.astype(BF16)
+
+    def plain_decode(values, stage, h, d, summed):
+        return values.astype(F32)
+
     drain = reduce_scatter(
-        regrouped, wide_s1, wide_r1, wide_s2, wide_r2, nothing, nothing, keep(target, dir_all)
+        regrouped, power_code, power_decode, bounds_turn, bounds_end, keep(target, dir_all)
     )
     gather_and_multiply(dir_all, fit_one, (nothing, drain, nothing))
 
@@ -378,7 +434,7 @@
     exchange_start(0, 0)
 
     drain = reduce_scatter(
-        fit_low, low_s1, low_r1, low_s2, low_r2,
+        fit_low, plain_code, plain_decode,
         functools.partial(exchange_turn, 0), nothing, keep(image, image_all),
     )
     sums = exchange_sum(0, 1)
@@ -430,7 +486,7 @@
 
     ex_s[3, 0] = jnp.zeros_like(ex_s[3, 0])
     drain = reduce_scatter(
-        fit_low, low_s1, low_r1, low_s2, low_r2,
+        fit_low, plain_code, plain_decode,
         functools.partial(exchange_turn, 2), second_weights, residual_two,
     )
     exchange_start(3, 0)
@@ -456,7 +512,7 @@
         ),
         in_specs=[
             pl.BlockSpec(memory_space=pltpu.SMEM),
-            vmem,
+            pl.BlockSpec(memory_space=pl.ANY),
             pl.BlockSpec(memory_space=pl.ANY),
         ],
         out_specs=(vmem, vmem),
@@ -471,17 +527,15 @@
             pltpu.VMEM((2, SIDE, half, evals), F32),
             pltpu.VMEM((block, evals), F32),
             pltpu.VMEM((block, evals), F32),
-            pltpu.VMEM(first, F32),
-            pltpu.VMEM(first, F32),
-            pltpu.VMEM(second, F32),
-            pltpu.VMEM(second, F32),
             pltpu.VMEM(first, BF16),
             pltpu.VMEM(first, BF16),
             pltpu.VMEM(second, BF16),
             pltpu.VMEM(second, BF16),
-            pltpu.VMEM((4, 2, 8, evals), F32),
-            pltpu.VMEM((4, 2, SIDE - 1, 8, evals), F32),
+            pltpu.VMEM((6, 2, 8, evals), F32),
+            pltpu.VMEM((6, 2, SIDE - 1, 8, evals), F32),
+            pltpu.VMEM(margins.shape, BF16),
             pltpu.SemaphoreType.DMA((LOADS,)),
+            pltpu.SemaphoreType.DMA(()),
             pltpu.SemaphoreType.DMA((max(cols_size - 1, 1),)),
             pltpu.SemaphoreType.DMA((max(cols_size - 1, 1),)),
             pltpu.SemaphoreType.DMA((2, 2, 6)),
@@ -492,8 +546,8 @@
             pltpu.SemaphoreType.DMA((2, 2, 2)),
             pltpu.SemaphoreType.DMA((2, 2, 6)),
             pltpu.SemaphoreType.DMA((2, 2, 6)),
-            pltpu.SemaphoreType.DMA((4, 2, SIDE - 1)),
-            pltpu.SemaphoreType.DMA((4, 2, SIDE - 1)),
+            pltpu.SemaphoreType.DMA((6, 2, SIDE - 1)),
+            pltpu.SemaphoreType.DMA((6, 2, SIDE - 1)),
         ],
         compiler_params=pltpu.CompilerParams(
             collective_id=0, has_side_effects=True, vmem_limit_bytes=66_000_000

time: 179 us -> 161 us (0.90)
  Pallas kernels: 174 us -> 156 us
    pallas_call x1, Pallas kernels: 174 us -> 156 us  [per_device(): pl.pallas_call(functools.partial(fit, cols_size), out_shape=(jax.ShapeDty...]
where the time goes in v2:
time: 161 us
  Pallas kernels  156 us (97%)
  local copies, waits for them, and re-layouts  3.07 us (2%)
    pallas_call x1, Pallas kernels, per_device(): pl.pallas_call(functools.partial(fit, cols_size), out_shape=(jax.ShapeDty...  156 us

profile of v2, /device:TPU:0, one launch (start us, length us, event | category | flops | bytes accessed | tf_op | source)
XLA Modules:
  0.0 160.5 jit_solution(5256801063533916201)
XLA Ops:
  1.3 156.2 %shard_map.50 = (f32[512,256]{1,0:T(8,128)}, f32[1,256]{1,0:T(1,128)}) custom-call(f32[1,1]{1,0:T(1,128)} %bitcast.2.ridge_ref, bf16[128,2048]{1,0:T(8,128)(2,1)} %margins_hbm.1, bf16[1024,8192]{1,0:T(8,128)(2,1)} %mask_ref.1), custom_call_target="tpu_custom_call" | custom-call | tf_op jit(solution)/shard_map/pallas_call | solution.py:507
  157.5 1.9 %copy.8 = f32[512,256]{1,0:T(8,128)} copy(f32[512,256]{1,0:T(8,128)} %get-tuple-element.8) | data formatting | bytes 1048576
  159.3 1.2 copy.9

commit v3 on v2

--- a/solution.py
+++ b/solution.py
@@ -22,15 +22,16 @@
 def fit(
     cols_size, ridge_ref, margins_hbm, mask_ref, w_ref, rn_ref,
     design, regrouped, dir_all, image_all, fit_one, fit_two, fit_low, own, target, image,
-    s1, r1, s2, r2, ex_s, ex_r, margins,
-    load_sem, margins_sem, m_send, m_recv, s1_send, s1_recv, s2_send, s2_recv,
+    s1, r1, s2, r2, ex_s, ex_r, margins, w_kept, last_s, last_r,
+    load_sem, margins_sem, w_sem, last_send, last_recv, m_send, m_recv, s1_send, s1_recv, s2_send, s2_recv,
     a1_send, a1_recv, a2_send, a2_recv, ex_send, ex_recv,
 ):
     row = lax.axis_index("rows")
     col = lax.axis_index("cols")
     x, z = lax.div(row, SIDE), lax.rem(row, SIDE)
     depth, examples = design.shape
-    block = examples // (SIDE * SIDE)
+    rows_size = SIDE * SIDE
+    block = examples // rows_size
     half = block // 2
     quarter = half // 2
     evals = target.shape[1]
@@ -58,17 +59,17 @@
 
     margins_load = pltpu.make_async_copy(margins_hbm, margins, margins_sem)
     margins_load.start()
-    for i in range(LOADS):
-        load(i).start()
-
     barrier = pltpu.get_barrier_semaphore()
-    for i in range(1, SIDE):
-        for peer in line(i):
-            pl.semaphore_signal(barrier, inc=1, device_id={"rows": peer}, device_id_type=MESH)
+    for i in range(1, rows_size):
+        peer = lax.rem(row + i, rows_size)
+        pl.semaphore_signal(barrier, inc=1, device_id={"rows": peer}, device_id_type=MESH)
     for i in range(1, cols_size):
         peer = lax.rem(col + i, cols_size)
         pl.semaphore_signal(barrier, inc=1, device_id={"cols": peer}, device_id_type=MESH)
-    pl.semaphore_wait(barrier, 2 * (SIDE - 1) + cols_size - 1)
+    margins_load.wait()
+    for i in range(LOADS):
+        load(i).start()
+    pl.semaphore_wait(barrier, rows_size + cols_size - 2)
 
     def hand_over(i):
         peer = lax.rem(col + i, cols_size)
@@ -81,7 +82,6 @@
             device_id_type=MESH,
         )
 
-    margins_load.wait()
     for i in range(1, cols_size):
         hand_over(i).start()
     regrouped[pl.ds(pl.multiple_of(col * per, per), per)] = margins[
@@ -108,7 +108,7 @@
             preferred_element_type=F32,
         )
 
-    def reduce_scatter(operand, encode, decode, after_far, after_own, done):
+    def reduce_scatter(operand, encode, decode, hooks, done):
         def send1(h, d, slot):
             return pltpu.make_async_remote_copy(
                 s1.at[h, d, slot],
@@ -157,12 +157,15 @@
             h, d, s = parts(i)
             send_block(h, d, s, 1 - (s - d) * (s - d), 2 - s, None, None)
 
-        @pl.loop(0, 8)
-        def _(i):
-            h, k = lax.rem(i, 2), lax.div(i, 2)
-            own[h, k] = partial(operand, h, c1(h), c2(h) + k)
-
-        after_far()
+        def own_blocks(low):
+            @pl.loop(0, 4)
+            def _(i):
+                h, k = lax.rem(i, 2), low + lax.div(i, 2)
+                own[h, k] = partial(operand, h, c1(h), c2(h) + k)
+
+        hooks[0]()
+        own_blocks(2)
+        hooks[1]()
 
         @pl.loop(0, 8)
         def _(i):
@@ -170,7 +173,17 @@
             add = 1 - (s - d) * (s - d)
             send_block(h, d, 2 + s, 1 - add, d + 2 * (1 - s), add, d)
 
-        after_own()
+        own_blocks(0)
+        hooks[2]()
+
+        @pl.loop(0, 8)
+        def _(i):
+            h, d, s = parts(i)
+            add = d
+            d = d + s - 2 * d * s
+            send_block(h, d, 4 + s, s * 0, 3 * (1 - s), add, 3 - d)
+
+        hooks[3]()
 
         def collect(h, k):
             for d in (0, 1):
@@ -187,12 +200,6 @@
             for d in (0, 1):
                 s2[h, d, 0] = encode(part(h, 2, d), 2, h, d, 0)
                 send2(h, d, 0).start()
-
-        @pl.loop(0, 8)
-        def _(i):
-            h, d, s = parts(i)
-            add = s + d - 2 * s * d
-            send_block(h, d, 4 + s, s * 0, 3 * (1 - s), add, 3 - d)
 
         for d, k in ((0, 1), (1, 3)):
             for h in (0, 1):
@@ -264,8 +271,10 @@
         send1, send2 = gather_steps(everything)
         for d in (0, 1):
             send1(h, d, 0).start()
-        for d in (0, 1):
-            send2(h, d, 0).start()
+        if h == 1:
+            for half_of in (1, 0):
+                for d in (0, 1):
+                    send2(half_of, d, 0).start()
 
     def gather_and_multiply(everything, result, meanwhile):
         send1, send2 = gather_steps(everything)
@@ -420,22 +429,25 @@
         return values.astype(F32)
 
     drain = reduce_scatter(
-        regrouped, power_code, power_decode, bounds_turn, bounds_end, keep(target, dir_all)
+        regrouped, power_code, power_decode, (nothing, bounds_turn, nothing, bounds_end),
+        keep(target, dir_all),
     )
     gather_and_multiply(dir_all, fit_one, (nothing, drain, nothing))
 
     fit_low[...] = fit_one[...].astype(BF16)
 
-    ex_s[0, 0] = jnp.zeros_like(ex_s[0, 0])
-    ex_s[0, 0, pl.ds(0, 1)] = total(target[...] * target[...])
-    ex_s[0, 0, pl.ds(1, 1)] = total(fit_one[...] * fit_low[...].astype(F32)) + ridge * total(
-        low(target[...]) * target[...]
-    )
-    exchange_start(0, 0)
+    def first_sums():
+        ex_s[0, 0] = jnp.zeros_like(ex_s[0, 0])
+        ex_s[0, 0, pl.ds(0, 1)] = total(target[...] * target[...])
+        ex_s[0, 0, pl.ds(1, 1)] = total(fit_one[...] * fit_low[...].astype(F32)) + ridge * total(
+            low(target[...]) * target[...]
+        )
+        exchange_start(0, 0)
 
     drain = reduce_scatter(
         fit_low, plain_code, plain_decode,
-        functools.partial(exchange_turn, 0), nothing, keep(image, image_all),
+        (first_sums, nothing, functools.partial(exchange_turn, 0), nothing),
+        keep(image, image_all),
     )
     sums = exchange_sum(0, 1)
     first_norms = sums[0:1]
@@ -458,21 +470,25 @@
     fit_two[...] = (1 + beta - alpha_one * ridge) * fit_one[...] - alpha_one * fit_two[...]
     fit_low[...] = fit_two[...].astype(BF16)
 
-    ex_s[2, 0] = jnp.zeros_like(ex_s[2, 0])
-    residual = residual_one()
-    direction = residual + beta * target[...]
-    w_ref[...] = alpha_one * target[...]
-    image[...] = residual
-    target[...] = direction
-    ex_s[2, 0, pl.ds(0, 1)] = total(fit_two[...] * fit_low[...].astype(F32)) + ridge * total(
-        low(target[...]) * target[...]
-    )
-    exchange_start(2, 0)
+    def second_sums():
+        ex_s[2, 0] = jnp.zeros_like(ex_s[2, 0])
+        residual = residual_one()
+        direction = residual + beta * target[...]
+        w_kept[...] = alpha_one * target[...]
+        image[...] = residual
+        target[...] = direction
+        ex_s[2, 0, pl.ds(0, 1)] = total(fit_two[...] * fit_low[...].astype(F32)) + ridge * total(
+            low(target[...]) * target[...]
+        )
+        exchange_start(2, 0)
+
+    w_store = pltpu.make_async_copy(w_kept, w_ref, w_sem)
 
     def second_weights():
         alpha_two = norm_one / exchange_sum(2, 1)[0:1]
         ex_s[3, 1, pl.ds(0, 1)] = alpha_two
-        w_ref[...] = w_ref[...] + alpha_two * target[...]
+        w_kept[...] = w_kept[...] + alpha_two * target[...]
+        w_store.start()
 
     def residual_two(h, sums):
         alpha_two = ex_s[3, 1, pl.ds(0, 1)]
@@ -482,18 +498,33 @@
             left = image[rows] - alpha_two * (sums[j] + ridge * target[rows])
             square = total(left * left)
             squares = square if squares is None else squares + square
-        ex_s[3, 0, pl.ds(h, 1)] = squares
-
-    ex_s[3, 0] = jnp.zeros_like(ex_s[3, 0])
+        last_s[...] = squares if h == 0 else last_s[...] + squares
+
     drain = reduce_scatter(
         fit_low, plain_code, plain_decode,
-        functools.partial(exchange_turn, 2), second_weights, residual_two,
+        (second_sums, nothing, functools.partial(exchange_turn, 2), second_weights),
+        residual_two,
     )
-    exchange_start(3, 0)
-    exchange_turn(3)
+
+    def last(i):
+        return pltpu.make_async_remote_copy(
+            last_s,
+            last_r.at[i - 1],
+            last_send.at[i - 1],
+            last_recv.at[i - 1],
+            device_id={"rows": lax.rem(row + i, rows_size)},
+            device_id_type=MESH,
+        )
+
+    for i in range(1, rows_size):
+        last(i).start()
     drain()
-    squares = exchange_sum(3, 1)
-    rn_ref[...] = jnp.sqrt((squares[0:1] + squares[1:2]) / first_norms)
+    w_store.wait()
+    squares = last_s[...]
+    for i in range(1, rows_size):
+        last(i).wait()
+        squares = squares + last_r[i - 1]
+    rn_ref[...] = jnp.sqrt(squares / first_norms)
 
 
 def per_device(cols_size, margins, subset_masks, ridge_param):
@@ -515,7 +546,7 @@
             pl.BlockSpec(memory_space=pl.ANY),
             pl.BlockSpec(memory_space=pl.ANY),
         ],
-        out_specs=(vmem, vmem),
+        out_specs=(pl.BlockSpec(memory_space=pl.ANY), vmem),
         scratch_shapes=[
             pltpu.VMEM((depth, examples), BF16),
             pltpu.VMEM((depth, evals), BF16),
@@ -534,8 +565,14 @@
             pltpu.VMEM((6, 2, 8, evals), F32),
             pltpu.VMEM((6, 2, SIDE - 1, 8, evals), F32),
             pltpu.VMEM(margins.shape, BF16),
+            pltpu.VMEM((block, evals), F32),
+            pltpu.VMEM((1, evals), F32),
+            pltpu.VMEM((SIDE * SIDE - 1, 1, evals), F32),
             pltpu.SemaphoreType.DMA((LOADS,)),
             pltpu.SemaphoreType.DMA(()),
+            pltpu.SemaphoreType.DMA(()),
+            pltpu.SemaphoreType.DMA((SIDE * SIDE - 1,)),
+            pltpu.SemaphoreType.DMA((SIDE * SIDE - 1,)),
             pltpu.SemaphoreType.DMA((max(cols_size - 1, 1),)),
             pltpu.SemaphoreType.DMA((max(cols_size - 1, 1),)),
             pltpu.SemaphoreType.DMA((2, 2, 6)),

time: 161 us -> 155 us (0.963)
  Pallas kernels: 156 us -> 150 us
    pallas_call x1, Pallas kernels: 156 us -> 150 us  [per_device(): pl.pallas_call(functools.partial(fit, cols_size), out_shape=(jax.ShapeDty...]
where the time goes in v3:
time: 155 us; the launch traced here: 154 us
  Pallas kernels  150 us (97%)
  local copies, waits for them, and re-layouts  3.07 us (2%)
    pallas_call x1, Pallas kernels, per_device(): pl.pallas_call(functools.partial(fit, cols_size), out_shape=(jax.ShapeDty...  150 us

profile of v3, /device:TPU:0, one launch (start us, length us, event | category | flops | bytes accessed | tf_op | source)
XLA Modules:
  0.0 154.5 jit_solution(15799232843770087948)
XLA Ops:
  1.3 150.1 %shard_map.50 = (f32[512,256]{1,0:T(8,128)}, f32[1,256]{1,0:T(1,128)}) custom-call(f32[1,1]{1,0:T(1,128)} %bitcast.2.ridge_ref, bf16[128,2048]{1,0:T(8,128)(2,1)} %margins_hbm.1, bf16[1024,8192]{1,0:T(8,128)(2,1)} %mask_ref.1), custom_call_target="tpu_custom_call" | custom-call | tf_op jit(solution)/shard_map/pallas_call | solution.py:538
  151.4 1.9 %copy.8 = f32[512,256]{1,0:T(8,128)} copy(f32[512,256]{1,0:T(8,128)} %get-tuple-element.8) | data formatting | bytes 1048576
  153.3 1.2 copy.9

commit v4 on v3

--- a/solution.py
+++ b/solution.py
@@ -82,7 +82,7 @@
             device_id_type=MESH,
         )
 
-    for i in range(1, cols_size):
+    for i in sorted(range(1, cols_size), key=lambda i: abs(i - cols_size // 2)):
         hand_over(i).start()
     regrouped[pl.ds(pl.multiple_of(col * per, per), per)] = margins[
         :, pl.ds(pl.multiple_of(col * evals, evals), evals)
@@ -157,6 +157,16 @@
             h, d, s = parts(i)
             send_block(h, d, s, 1 - (s - d) * (s - d), 2 - s, None, None)
 
+        def collect(h, k):
+            for d in (0, 1):
+                slot = FIRST_SLOT[d][k]
+                summed = int((d, slot) in ((0, 2), (0, 5), (1, 3), (1, 4)))
+                send1(h, d, slot).wait_recv()
+                own[h, k] = own[h, k] + decode(r1[h, d, slot], 1, h, d, summed)
+
+        def part(h, k, j):
+            return own[h, k, pl.ds(j * quarter, quarter)]
+
         def own_blocks(low):
             @pl.loop(0, 4)
             def _(i):
@@ -175,6 +185,12 @@
 
         own_blocks(0)
         hooks[2]()
+        for h in (0, 1):
+            collect(h, 2)
+            for d in (0, 1):
+                s2[h, d, 0] = encode(part(h, 2, d), 2, h, d, 0)
+                send2(h, d, 0).start()
+
 
         @pl.loop(0, 8)
         def _(i):
@@ -184,22 +200,6 @@
             send_block(h, d, 4 + s, s * 0, 3 * (1 - s), add, 3 - d)
 
         hooks[3]()
-
-        def collect(h, k):
-            for d in (0, 1):
-                slot = FIRST_SLOT[d][k]
-                summed = int((d, slot) in ((0, 2), (0, 5), (1, 3), (1, 4)))
-                send1(h, d, slot).wait_recv()
-                own[h, k] = own[h, k] + decode(r1[h, d, slot], 1, h, d, summed)
-
-        def part(h, k, j):
-            return own[h, k, pl.ds(j * quarter, quarter)]
-
-        for h in (0, 1):
-            collect(h, 2)
-            for d in (0, 1):
-                s2[h, d, 0] = encode(part(h, 2, d), 2, h, d, 0)
-                send2(h, d, 0).start()
 
         for d, k in ((0, 1), (1, 3)):
             for h in (0, 1):
@@ -429,10 +429,10 @@
         return values.astype(F32)
 
     drain = reduce_scatter(
-        regrouped, power_code, power_decode, (nothing, bounds_turn, nothing, bounds_end),
+        regrouped, power_code, power_decode, (nothing, bounds_turn, bounds_end, nothing),
         keep(target, dir_all),
     )
-    gather_and_multiply(dir_all, fit_one, (nothing, drain, nothing))
+    gather_and_multiply(dir_all, fit_one, (drain, nothing, nothing))
 
     fit_low[...] = fit_one[...].astype(BF16)
 
@@ -460,11 +460,7 @@
     ex_s[1, 0, pl.ds(0, 1)] = total(residual_one() * residual_one())
     exchange_start(1, 0)
 
-    def middle():
-        exchange_turn(1)
-        drain()
-
-    gather_and_multiply(image_all, fit_two, (nothing, middle, nothing))
+    gather_and_multiply(image_all, fit_two, (drain, functools.partial(exchange_turn, 1), nothing))
     norm_one = exchange_sum(1, 1)[0:1]
     beta = norm_one / first_norms
     fit_two[...] = (1 + beta - alpha_one * ridge) * fit_one[...] - alpha_one * fit_two[...]

time: 155 us -> 152 us (0.981)
  Pallas kernels: 150 us -> 147 us
    pallas_call x1, Pallas kernels: 150 us -> 147 us  [per_device(): pl.pallas_call(functools.partial(fit, cols_size), out_shape=(jax.ShapeDty...]
where the time goes in v4:
time: 152 us
  Pallas kernels  147 us (97%)
  local copies, waits for them, and re-layouts  3.07 us (2%)
    pallas_call x1, Pallas kernels, per_device(): pl.pallas_call(functools.partial(fit, cols_size), out_shape=(jax.ShapeDty...  147 us
    unnamed x2, local copies, waits for them, and re-layouts  3.07 us

profile of v4, /device:TPU:0, one launch (start us, length us, event | category | flops | bytes accessed | tf_op | source)
XLA Modules:
  0.0 151.6 jit_solution(10873563813422833185)
XLA Ops:
  1.3 147.3 %shard_map.50 = (f32[512,256]{1,0:T(8,128)}, f32[1,256]{1,0:T(1,128)}) custom-call(f32[1,1]{1,0:T(1,128)} %bitcast.2.ridge_ref, bf16[128,2048]{1,0:T(8,128)(2,1)} %margins_hbm.1, bf16[1024,8192]{1,0:T(8,128)(2,1)} %mask_ref.1), custom_call_target="tpu_custom_call" | custom-call | tf_op jit(solution)/shard_map/pallas_call | solution.py:534
  148.6 1.9 %copy.8 = f32[512,256]{1,0:T(8,128)} copy(f32[512,256]{1,0:T(8,128)} %get-tuple-element.8) | data formatting | bytes 1048576
  150.4 1.2 copy.9

commit v5 on v4

--- a/solution.py
+++ b/solution.py
@@ -312,12 +312,12 @@
                 send1(h, d, 1).wait_recv()
             for d in (0, 1):
                 send2(h, d, 3).start()
+        for h in (0, 1):
+            for d in (0, 1):
+                send2(h, d, 0).wait_recv()
+            send2(h, 0, 4).start()
         multiply([(0, 2)])
         meanwhile[1]()
-        for h in (0, 1):
-            for d in (0, 1):
-                send2(h, d, 0).wait_recv()
-            send2(h, 0, 4).start()
         multiply([(-1, 0), (1, 0)])
         for h in (0, 1):
             for slot in (1, 2):
@@ -333,11 +333,10 @@
             send2(h, 1, 5).start()
         multiply([(-1, 2), (1, 2)])
         meanwhile[2]()
-        for slot in (4, 5):
+        for d, slot in ((0, 4), (1, 4), (0, 5), (1, 5)):
             for h in (0, 1):
-                for d in (0, 1):
-                    send2(h, d, slot).wait_recv()
-            multiply([(2, GATHER_PASS[0][slot - 4]), (2, GATHER_PASS[1][slot - 4])])
+                send2(h, d, slot).wait_recv()
+            multiply([(2, GATHER_PASS[d][slot - 4])])
         for h in (0, 1):
             for d in (0, 1):
                 for slot in range(2):

time: 152 us -> 151 us (level)
  no operation moved by 1% of the time
where the time goes in v5:
time: 151 us
  Pallas kernels  146 us (97%)
  local copies, waits for them, and re-layouts  3.07 us (2%)
    pallas_call x1, Pallas kernels, per_device(): pl.pallas_call(functools.partial(fit, cols_size), out_shape=(jax.ShapeDty...  146 us
    unnamed x2, local copies, waits for them, and re-layouts  3.07 us

profile of v5, /device:TPU:0, one launch (start us, length us, event | category | flops | bytes accessed | tf_op | source)
XLA Modules:
  0.0 150.8 jit_solution(6620069104815996660)
XLA Ops:
  1.3 146.5 %shard_map.50 = (f32[512,256]{1,0:T(8,128)}, f32[1,256]{1,0:T(1,128)}) custom-call(f32[1,1]{1,0:T(1,128)} %bitcast.2.ridge_ref, bf16[128,2048]{1,0:T(8,128)(2,1)} %margins_hbm.1, bf16[1024,8192]{1,0:T(8,128)(2,1)} %mask_ref.1), custom_call_target="tpu_custom_call" | custom-call | tf_op jit(solution)/shard_map/pallas_call | solution.py:533
  147.7 1.9 %copy.8 = f32[512,256]{1,0:T(8,128)} copy(f32[512,256]{1,0:T(8,128)} %get-tuple-element.8) | data formatting | bytes 1048576
  149.6 1.2 copy.9
